TPU v7x, 32 devices: a whole 2x2x4 slice. The times are simulated.
32 devices in a mesh: row: 4 (over y, core), col: 8 (over z, x).
Axes of the slice: x: 2, y: 2, z: 4, core: 2. Of those that a mesh axis runs over, the one named last changes fastest.
Arguments:
- matrix: float32 [16384, 16384], P('row', 'col'), as said below
Outputs:
- hess_panel: float32 [16384, 8], P('row')
- reflectors: float32 [16384, 8], P('row')
- wy_products: float32 [16384, 8], P('row')
- wy_factor: float32 [8, 8], replicated
Inputs may be any that keep to these rules, and one draw needn't show every extreme that they name: Entries matrix[i+1, i] lie within 2.5 +- 6 / sqrt(16384); every other entry within +- 6 / sqrt(16384).
All inputs are finite; a program needn't handle non-finite values.
Results may differ from a plain program's by a relative error of at most 0.0003.
Values sent between devices are 32-bit elements; how exact they have to be, the bound alone decides.
A program may use at most 128 MiB of HBM per device.

v0:
```python
import jax
import jax.numpy as jnp
from jax import lax
from jax.sharding import PartitionSpec as P

NB = 8


def spread(value, axis, root):
    mine = lax.axis_index(axis) == root
    return lax.psum(jnp.where(mine, value, jnp.zeros_like(value)), axis)


def shards(matrix):
    exact = lax.Precision.HIGHEST
    rows_local, cols_local = matrix.shape
    row_ids = lax.axis_index("row") * rows_local + lax.iota(jnp.int32, rows_local)
    panel = spread(matrix[:, :NB], "col", 0)
    top_ids = lax.iota(jnp.int32, NB + 1)
    picker = (row_ids[None, :] == top_ids[:, None]).astype(jnp.float32)
    refl = jnp.zeros((rows_local, NB), jnp.float32)
    wy_prod = jnp.zeros((rows_local, NB), jnp.float32)
    factor = jnp.zeros((NB, NB), jnp.float32)
    refl_top = jnp.zeros((NB + 1, NB), jnp.float32)
    gram = jnp.zeros((NB, NB), jnp.float32)
    columns = []
    for column in range(NB):
        current = panel[:, column] - jnp.dot(wy_prod, refl_top[column], precision=exact)
        if column > 0:
            inner = lax.psum(jnp.dot(current, refl, precision=exact), "row")
            current = current - jnp.dot(
                refl, jnp.dot(inner, factor, precision=exact), precision=exact
            )
        below = jnp.where(row_ids > column, current, jnp.float32(0.0))
        sumsq, leading = lax.psum(
            (
                jnp.sum(below * below),
                jnp.sum(jnp.where(row_ids == column + 1, current, jnp.float32(0.0))),
            ),
            "row",
        )
        masked = jnp.where(row_ids > column, current, jnp.float32(0.0))
        length = jnp.sqrt(sumsq)
        orient = jnp.where(leading >= 0, jnp.float32(1.0), jnp.float32(-1.0))
        pivot_value = -orient * length
        vector = masked + jnp.where(row_ids == column + 1, orient * length, jnp.float32(0.0))
        vector = vector / jnp.sqrt(length * (length + jnp.abs(leading)))
        start = lax.axis_index("col") * cols_local
        received = spread(vector, "row", start // rows_local)
        piece = lax.dynamic_slice_in_dim(received, start % rows_local, cols_local, 0)
        coupling, vec_top = lax.psum(
            (jnp.dot(vector, refl, precision=exact), jnp.dot(picker, vector, precision=exact)),
            "row",
        )
        image = lax.psum(jnp.dot(matrix, piece, precision=exact), "col")
        new_y = image - jnp.dot(wy_prod, coupling, precision=exact)
        new_t = -jnp.dot(factor, coupling, precision=exact)
        factor = factor.at[:, column].set(new_t).at[column, column].set(jnp.float32(1.0))
        gram = (
            gram.at[:, column]
            .set(coupling)
            .at[column, :]
            .set(coupling)
            .at[column, column]
            .set(jnp.float32(2.0))
        )
        wy_prod = wy_prod.at[:, column].set(new_y)
        refl = refl.at[:, column].set(vector)
        refl_top = refl_top.at[:, column].set(vec_top)
        columns.append(
            jnp.where(
                row_ids <= column,
                current,
                jnp.where(row_ids == column + 1, pivot_value, jnp.float32(0.0)),
            )
        )
    return (jnp.stack(columns, axis=1), refl, wy_prod, factor)


def solution(mesh):
    return jax.shard_map(
        shards,
        mesh=mesh,
        in_specs=(P("row", "col"),),
        out_specs=(P("row", None), P("row", None), P("row", None), P()),
        check_vma=False,
    )
```

profile of v0, /device:TPU:0, one launch (start us, length us, event | category | flops | bytes accessed | tf_op | source)
XLA Modules:
  0.0 897.8 jit_solution(13445658246605330233)
XLA Ops:
  15.5 101.1 %all-reduce.22.cloned.1.call-done = f32[4096,8]{1,0:T(8,128)} async-done(((f32[4096,8]{1,0:T(8,128)}), f32[4096,8]{1,0:T(8,128)}) %all-reduce.22.cloned.1.call-update) | async-done | bytes 131088 | tf_op jit(solution)/shard_map/psum | solution.py:11
  116.7 15.4 %slice_reduce_fusion = (f32[4096]{0:T(1024)S(1)}, f32[4096]{0:T(1024)S(1)}, f32[4096]{0:T(1024)S(1)}, f32[4096]{0:T(1024)S(1)}, f32[4096]{0:T(1024)S(1)}, /*inde...) fusion(f32[4096,8]{1,0:T(8,128)} %all-reduce.22.cloned.1.call-done), kind=kLoop, calls=%fused_computation | loop fusion | bytes 262144 | tf_op jit(solution)/shard_map/slice | solution.py:28
  133.3 6.8 all-reduce.19
  143.5 10.6 %all-reduce.18 = (f32[4096]{0:T(1024)S(1)}, f32[8]{0:T(128)S(1)}, f32[9]{0:T(128)S(1)}) all-reduce(f32[4096]{0:T(1024)S(1)} %broadcast_select_fusion.19, f32[8]{0:T(128)S(1)} %convolution_bitcast_fusion.36, f32[9]{0:T(128)S(1)} %convolution_bitcast_fusion.35), channel_id=1, replica_groups=mesh['row'=4,'col'=8] {'row'}, use_global_device_ids=true, to_apply=%region_6.7 | all-reduce | flops 4113 | bytes 32904 | tf_op jit(solution)/shard_map/psum | solution.py:11
  154.1 30.7 %fusion.122 = f32[1,4096]{1,0:T(1,128)S(1)} fusion(f32[2048,1]{0,1:T(1,128)S(1)} %bitcast.507, f32[4096,2048]{1,0:T(8,128)} %param.79), kind=kOutput, calls=%fused_computation.248 | convolution fusion | flops 100663296 | bytes 33579008 | tf_op jit(solution)/shard_map/dot_general | solution.py:55
  184.7 35.8 %psum.389 = f32[4096]{0:T(1024)S(1)} all-reduce(f32[4096]{0:T(1024)S(1)} %bitcast.450), channel_id=1, replica_groups=mesh['row'=4,'col'=8] {'col'}, use_global_device_ids=true, to_apply=%region_7.8 | all-reduce | flops 4096 | bytes 32768 | tf_op jit(solution)/shard_map/psum | solution.py:55
  241.9 10.3 %all-reduce.16 = (f32[4096]{0:T(1024)S(1)}, f32[8]{0:T(128)S(1)}, f32[9]{0:T(128)S(1)}) all-reduce(f32[4096]{0:T(1024)S(1)} %broadcast_select_fusion.17, f32[8]{0:T(128)S(1)} %convolution_bitcast_fusion.33, f32[9]{0:T(128)S(1)} %convolution_bitcast_fusion.32), channel_id=1, replica_groups=mesh['row'=4,'col'=8] {'row'}, use_global_device_ids=true, to_apply=%region_16.17 | all-reduce | flops 4113 | bytes 32904 | tf_op jit(solution)/shard_map/psum | solution.py:11
  253.3 30.7 %fusion.123 = f32[1,4096]{1,0:T(1,128)S(1)} fusion(f32[2048,1]{0,1:T(1,128)S(1)} %bitcast.508, f32[4096,2048]{1,0:T(8,128)} %param.79), kind=kOutput, calls=%fused_computation.249 | convolution fusion | flops 100663296 | bytes 33579008 | tf_op jit(solution)/shard_map/dot_general | solution.py:55
  284.0 33.0 %psum.396 = f32[4096]{0:T(1024)S(1)} all-reduce(f32[4096]{0:T(1024)S(1)} %bitcast.451), channel_id=1, replica_groups=mesh['row'=4,'col'=8] {'col'}, use_global_device_ids=true, to_apply=%region_17.18 | all-reduce | flops 4096 | bytes 32768 | tf_op jit(solution)/shard_map/psum | solution.py:55
  326.6 7.3 all-reduce.15
  337.3 10.6 %all-reduce.14 = (f32[4096]{0:T(1024)S(1)}, f32[8]{0:T(128)S(1)}, f32[9,1]{0,1:T(1,128)S(1)}) all-reduce(f32[4096]{0:T(1024)S(1)} %get-tuple-element.558, f32[8]{0:T(128)S(1)} %convolution_bitcast_fusion.30, f32[9,1]{0,1:T(1,128)S(1)} %convolution_bitcast_fusion.29), channel_id=1, replica_groups=mesh['row'=4,'col'=8] {'row'}, use_global_device_ids=true, to_apply=%region_26.27 | all-reduce | flops 4113 | bytes 32904 | tf_op jit(solution)/shard_map/psum | solution.py:11
  350.0 30.7 %fusion.125 = f32[1,4096]{1,0:T(1,128)S(1)} fusion(f32[2048,1]{0,1:T(1,128)S(1)} %bitcast.509, f32[4096,2048]{1,0:T(8,128)} %param.79), kind=kOutput, calls=%fused_computation.251 | convolution fusion | flops 100663296 | bytes 33579008 | tf_op jit(solution)/shard_map/dot_general | solution.py:55
  380.7 33.0 %psum.403 = f32[4096]{0:T(1024)S(1)} all-reduce(f32[4096]{0:T(1024)S(1)} %bitcast.452), channel_id=1, replica_groups=mesh['row'=4,'col'=8] {'col'}, use_global_device_ids=true, to_apply=%region_27.28 | all-reduce | flops 4096 | bytes 32768 | tf_op jit(solution)/shard_map/psum | solution.py:55
  432.9 10.3 %all-reduce.12 = (f32[4096]{0:T(1024)S(1)}, f32[8]{0:T(128)S(1)}, f32[9,1]{0,1:T(1,128)S(1)}) all-reduce(f32[4096]{0:T(1024)S(1)} %get-tuple-element.555, f32[8]{0:T(128)S(1)} %convolution_bitcast_fusion.27, f32[9,1]{0,1:T(1,128)S(1)} %convolution_bitcast_fusion.26), channel_id=1, replica_groups=mesh['row'=4,'col'=8] {'row'}, use_global_device_ids=true, to_apply=%region_36.37 | all-reduce | flops 4113 | bytes 32904 | tf_op jit(solution)/shard_map/psum | solution.py:11
  444.8 30.7 %fusion.127 = f32[1,4096]{1,0:T(1,128)S(1)} fusion(f32[2048,1]{0,1:T(1,128)S(1)} %bitcast.510, f32[4096,2048]{1,0:T(8,128)} %param.79), kind=kOutput, calls=%fused_computation.253 | convolution fusion | flops 100663296 | bytes 33579008 | tf_op jit(solution)/shard_map/dot_general | solution.py:55
  475.5 33.0 %psum.410 = f32[4096]{0:T(1024)S(1)} all-reduce(f32[4096]{0:T(1024)S(1)} %bitcast.453), channel_id=1, replica_groups=mesh['row'=4,'col'=8] {'col'}, use_global_device_ids=true, to_apply=%region_37.38 | all-reduce | flops 4096 | bytes 32768 | tf_op jit(solution)/shard_map/psum | solution.py:55
  517.8 7.3 all-reduce.11
  528.5 10.6 %all-reduce.10 = (f32[4096]{0:T(1024)S(1)}, f32[8]{0:T(128)S(1)}, f32[9,1]{0,1:T(1,128)S(1)}) all-reduce(f32[4096]{0:T(1024)S(1)} %get-tuple-element.552, f32[8]{0:T(128)S(1)} %convolution_bitcast_fusion.24, f32[9,1]{0,1:T(1,128)S(1)} %convolution_bitcast_fusion.23), channel_id=1, replica_groups=mesh['row'=4,'col'=8] {'row'}, use_global_device_ids=true, to_apply=%region_46.47 | all-reduce | flops 4113 | bytes 32904 | tf_op jit(solution)/shard_map/psum | solution.py:11
  541.0 30.7 %fusion.129 = f32[1,4096]{1,0:T(1,128)S(1)} fusion(f32[2048,1]{0,1:T(1,128)S(1)} %bitcast.511, f32[4096,2048]{1,0:T(8,128)} %param.79), kind=kOutput, calls=%fused_computation.255 | convolution fusion | flops 100663296 | bytes 33579008 | tf_op jit(solution)/shard_map/dot_general | solution.py:55
  571.7 33.0 %psum.417 = f32[4096]{0:T(1024)S(1)} all-reduce(f32[4096]{0:T(1024)S(1)} %bitcast.454), channel_id=1, replica_groups=mesh['row'=4,'col'=8] {'col'}, use_global_device_ids=true, to_apply=%region_47.48 | all-reduce | flops 4096 | bytes 32768 | tf_op jit(solution)/shard_map/psum | solution.py:55
  614.2 6.4 all-reduce.9
  624.0 10.3 %all-reduce.8 = (f32[4096]{0:T(1024)S(1)}, f32[8]{0:T(128)S(1)}, f32[9,1]{0,1:T(1,128)S(1)}) all-reduce(f32[4096]{0:T(1024)S(1)} %get-tuple-element.549, f32[8]{0:T(128)S(1)} %convolution_bitcast_fusion.21, f32[9,1]{0,1:T(1,128)S(1)} %convolution_bitcast_fusion.20), channel_id=1, replica_groups=mesh['row'=4,'col'=8] {'row'}, use_global_device_ids=true, to_apply=%region_56.57 | all-reduce | flops 4113 | bytes 32904 | tf_op jit(solution)/shard_map/psum | solution.py:11
  635.9 30.7 %fusion.131 = f32[1,4096]{1,0:T(1,128)S(1)} fusion(f32[2048,1]{0,1:T(1,128)S(1)} %bitcast.512, f32[4096,2048]{1,0:T(8,128)} %param.79), kind=kOutput, calls=%fused_computation.257 | convolution fusion | flops 100663296 | bytes 33579008 | tf_op jit(solution)/shard_map/dot_general | solution.py:55
  666.6 33.0 %psum.424 = f32[4096]{0:T(1024)S(1)} all-reduce(f32[4096]{0:T(1024)S(1)} %bitcast.455), channel_id=1, replica_groups=mesh['row'=4,'col'=8] {'col'}, use_global_device_ids=true, to_apply=%region_57.58 | all-reduce | flops 4096 | bytes 32768 | tf_op jit(solution)/shard_map/psum | solution.py:55
  708.8 7.3 all-reduce.7
  719.4 10.6 %all-reduce.6 = (f32[4096]{0:T(1024)S(1)}, f32[8]{0:T(128)S(1)}, f32[9,1]{0,1:T(1,128)S(1)}) all-reduce(f32[4096]{0:T(1024)S(1)} %get-tuple-element.546, f32[8]{0:T(128)S(1)} %convolution_bitcast_fusion.18, f32[9,1]{0,1:T(1,128)S(1)} %convolution_bitcast_fusion.17), channel_id=1, replica_groups=mesh['row'=4,'col'=8] {'row'}, use_global_device_ids=true, to_apply=%region_66.67 | all-reduce | flops 4113 | bytes 32904 | tf_op jit(solution)/shard_map/psum | solution.py:11
  732.0 30.7 %fusion.133 = f32[1,4096]{1,0:T(1,128)S(1)} fusion(f32[2048,1]{0,1:T(1,128)S(1)} %bitcast.513, f32[4096,2048]{1,0:T(8,128)} %param.79), kind=kOutput, calls=%fused_computation.259 | convolution fusion | flops 100663296 | bytes 33579008 | tf_op jit(solution)/shard_map/dot_general | solution.py:55
  762.7 33.0 %psum.431 = f32[4096]{0:T(1024)S(1)} all-reduce(f32[4096]{0:T(1024)S(1)} %bitcast.456), channel_id=1, replica_groups=mesh['row'=4,'col'=8] {'col'}, use_global_device_ids=true, to_apply=%region_67.68 | all-reduce | flops 4096 | bytes 32768 | tf_op jit(solution)/shard_map/psum | solution.py:55
  805.0 6.4 all-reduce.5
  813.8 10.3 %all-reduce.4 = (f32[4096]{0:T(1024)S(1)}, f32[8]{0:T(128)S(1)}) all-reduce(f32[4096]{0:T(1024)S(1)} %get-tuple-element.543, f32[8]{0:T(128)S(1)} %convolution_bitcast_fusion.15), channel_id=1, replica_groups=mesh['row'=4,'col'=8] {'row'}, use_global_device_ids=true, to_apply=%region_75.76 | all-reduce | flops 4104 | bytes 32832 | tf_op jit(solution)/shard_map/psum | solution.py:11
  825.9 30.7 %fusion.135 = f32[1,4096]{1,0:T(1,128)S(1)} fusion(f32[2048,1]{0,1:T(1,128)S(1)} %bitcast.506, f32[4096,2048]{1,0:T(8,128)} %param.79), kind=kOutput, calls=%fused_computation.261 | convolution fusion | flops 100663296 | bytes 33579008 | tf_op jit(solution)/shard_map/dot_general | solution.py:55
  856.6 33.0 %psum.438 = f32[4096]{0:T(1024)S(1)} all-reduce(f32[4096]{0:T(1024)S(1)} %bitcast.457), channel_id=1, replica_groups=mesh['row'=4,'col'=8] {'col'}, use_global_device_ids=true, to_apply=%region_76.77 | all-reduce | flops 4096 | bytes 32768 | tf_op jit(solution)/shard_map/psum | solution.py:55
  (192 shorter events, 112.8 us)
Async XLA Ops:
  7.2 109.5 %all-reduce.22.cloned.1.call-start = ((), (), s32[]{:S(2)}) async-start(), calls=%async_computation | async-start | bytes 4194304 | tf_op jit(solution)/shard_map/psum | solution.py:11
  824.9 65.9 %copy-start = (f32[4096,8]{0,1:T(8,128)}, f32[4096,8]{0,1:T(8,128)S(1)}, u32[]{:S(2)}) copy-start(f32[4096,8]{0,1:T(8,128)S(1)} %scatter.189) | copy-start | bytes 393220
  890.0 0.9 copy-start.1
Sparse Core Ops, SparseCore 0:
  11.6 105.0 all-reduce.21
where the time goes:
time: 907 us; the launch traced here: 898 us
  blocking collectives  444 us (49%)
  matrix products  265 us (29%)
  waiting for transfers between devices  101 us (11%)
  between operations  31.3 us (3%)
  local copies, waits for them, and re-layouts  28.4 us (3%)
  other arithmetic  27.4 us (3%)
    psum x8, blocking collectives, shards(): image = lax.psum(jnp.dot(matrix, piece, precision=exact), 'col')  267 us
    dot_general x8, matrix products, shards(): image = lax.psum(jnp.dot(matrix, piece, precision=exact), 'col')  246 us
    psum x1, waiting for transfers between devices, spread(): return lax.psum(jnp.where(mine, value, jnp.zeros_like(value)), axis)  101 us
    psum x8, blocking collectives, spread(): return lax.psum(jnp.where(mine, value, jnp.zeros_like(value)), axis)  83.5 us
    psum x8, blocking collectives, shards(): lax.psum((jnp.sum(below * below), jnp.sum(jnp.where(row_ids == column + 1...  54.1 us
    psum x7, blocking collectives, shards(): inner = lax.psum(jnp.dot(current, refl, precision=exact), 'row')  40.1 us
  transfers between devices with their start and end apart: 1, of which 1 were waited for; matrix products, arithmetic and copies ran while one was open for 1% of the time, Pallas kernels for 0%

commit v1 on v0

v1 whole, which is shorter than its diff:
```python
import functools

import jax
import jax.numpy as jnp
from jax import lax
from jax.experimental import pallas as pl
from jax.experimental.pallas import tpu as pltpu
from jax.sharding import PartitionSpec as P

NB = 8
LANES = 128
SUB = 8
CHUNK = LANES * SUB
BLOCK = 256
F32 = jnp.float32
BF16 = jnp.bfloat16


def kernel(
    nrow, ncol, a_hbm, hess_ref, refl_ref, wy_ref, fac_ref,
    a_ref, first_ref, pan_ref, mypan_ref, full_ref, vec_ref, part_ref, got_ref,
    out_ref, ymine_ref, dummy_ref,
    load_sem, first_sem, pan_send, pan_sem, rs_send, rs_sem, ag_send, ag_sem,
    y_send, y_sem,
):
    rows_local, cols_local = a_hbm.shape
    order = rows_local * nrow
    tiles = cols_local // LANES
    lines = rows_local // LANES
    owners = rows_local // CHUNK
    stride = ncol // owners
    row, col = lax.axis_index("row"), lax.axis_index("col")
    mine = col // stride
    is_owner = col - mine * stride == 0
    blocks = rows_local // BLOCK

    def wrap(value, bound):
        return jnp.where(value >= bound, value - bound, value)

    def peers_of_row(dr, act, skip):
        to_row = wrap(row + dr, nrow)
        for dc in range(1 if skip else 0, ncol):
            act(to_row, wrap(col + dc, ncol))

    def all_peers(act):
        def step(dr, carry):
            peers_of_row(dr, act, False)
            return carry

        lax.fori_loop(1, nrow, step, 0)
        peers_of_row(0, act, True)

    def block_load(i):
        span = pl.ds(i * BLOCK, BLOCK)
        return pltpu.make_async_copy(a_hbm.at[span], a_ref.at[span], load_sem.at[i])

    head = pltpu.make_async_copy(a_hbm.at[:, pl.ds(0, LANES)], first_ref, first_sem)

    @pl.when(col == 0)
    def _():
        head.start()

    for i in range(blocks):
        block_load(i).start()

    barrier = pltpu.get_barrier_semaphore()

    def greet(to_row, to_col):
        pl.semaphore_signal(
            barrier, inc=1, device_id=(to_row, to_col),
            device_id_type=pl.DeviceIdType.MESH,
        )

    all_peers(greet)
    pl.semaphore_wait(barrier, nrow * ncol - 1)

    def send(src, dst, send_sem, recv_sem, to_row, to_col):
        pltpu.make_async_remote_copy(
            src_ref=src, dst_ref=dst, send_sem=send_sem, recv_sem=recv_sem,
            device_id=(to_row, to_col), device_id_type=pl.DeviceIdType.MESH,
        ).start()

    def expect(ref, sem):
        pltpu.make_async_copy(ref, ref, sem).wait()

    @pl.when(col == 0)
    def _():
        head.wait()

        def turn(t, carry):
            block = first_ref[pl.ds(pl.multiple_of(t * LANES, LANES), LANES), :].T
            for k in range(NB):
                pan_ref[k, pl.ds(t, 1), :] = block[k : k + 1, :]
            return carry

        lax.fori_loop(0, lines, turn, 0)
        for q in range(1, owners):
            send(
                pan_ref.at[:, pl.ds(q * SUB, SUB)], mypan_ref, pan_send, pan_sem,
                row, jnp.int32(q * stride),
            )
        pltpu.make_async_copy(pan_ref.at[:, pl.ds(0, SUB)], mypan_ref, pan_sem).start()

    span = pl.ds(pl.multiple_of((row * owners + mine) * SUB, SUB), SUB)

    def gather(j):
        dst = full_ref.at[j, span]
        all_peers(
            lambda to_row, to_col: send(
                out_ref.at[j], dst, ag_send.at[j], ag_sem.at[j], to_row, to_col
            )
        )
        pltpu.make_async_copy(out_ref.at[j], dst, ag_sem.at[j]).start()

    @pl.when(is_owner)
    def _():
        expect(mypan_ref, pan_sem)
        out_ref[0] = mypan_ref[0]
        gather(0)

    ids = lax.broadcasted_iota(jnp.int32, (order // LANES, LANES), 0) * LANES
    ids = ids + lax.broadcasted_iota(jnp.int32, (order // LANES, LANES), 1)
    ones = jnp.ones((SUB, 2 * LANES), BF16)

    def total(value):
        return jnp.sum(jnp.sum(value, axis=0, keepdims=True), axis=1, keepdims=True)

    def fold(acc, t, j):
        high = acc.astype(BF16)
        low = (acc - high.astype(F32)).astype(BF16)
        both = jnp.concatenate([high, low], axis=1)
        res = lax.dot_general(
            ones, both, (((1,), (1,)), ((), ())), preferred_element_type=F32
        )
        part_ref[j, pl.ds(t, 1), :] = res[0:1, :]

    def matvec(j):
        base = col * tiles
        pieces = [
            jnp.broadcast_to(vec_ref[j, pl.ds(base + t, 1), :], (SUB, LANES))
            for t in range(tiles)
        ]

        def product(t):
            accs = []
            for s in range(LANES // SUB):
                at = pl.ds(pl.multiple_of(t * LANES + s * SUB, SUB), SUB)
                acc = a_ref[at, pl.ds(0, LANES)] * pieces[0]
                for p in range(1, tiles):
                    acc = acc + a_ref[at, pl.ds(p * LANES, LANES)] * pieces[p]
                accs.append(acc)
            return jnp.concatenate(accs, axis=0)

        per = BLOCK // LANES
        if j == 0:
            def loaded(i, carry):
                block_load(i).wait()
                for k in range(per):
                    fold(product(i * per + k), i * per + k, j)
                return carry

            lax.fori_loop(0, blocks, loaded, 0)
        else:
            def step(t, acc):
                fold(acc, t - 1, j)
                return product(t)

            fold(lax.fori_loop(1, lines, step, product(0)), lines - 1, j)

    factor = [[None] * NB for _ in range(NB)]
    local = pl.ds(pl.multiple_of(row * lines, SUB), lines)
    for j in range(NB):
        expect(full_ref.at[j], ag_sem.at[j])
        b = full_ref[j]
        if j > 0:
            inner = [total(vec_ref[k] * b) for k in range(j)]
            for m in range(j):
                weight = factor[0][m] * inner[0]
                for k in range(1, m + 1):
                    weight = weight + factor[k][m] * inner[k]
                b = b - vec_ref[m] * weight
        x = jnp.where(ids > j, b, F32(0.0))
        alpha = b[0:1, j + 1 : j + 2]
        norm = jnp.sqrt(total(x * x))
        signed = jnp.where(alpha >= 0, norm, -norm)
        u = x + jnp.where(ids == j + 1, signed, F32(0.0))
        u = u / jnp.sqrt(norm * (norm + jnp.abs(alpha)))
        vec_ref[j] = u
        matvec(j)
        for q in range(owners):
            @pl.when(jnp.logical_or(mine != q, jnp.logical_not(is_owner)))
            def _(q=q):
                send(
                    part_ref.at[j, pl.ds(q * SUB, SUB)], got_ref.at[j, col],
                    rs_send, rs_sem.at[j], row, jnp.int32(q * stride),
                )
        out_ref_h = jnp.where(ids <= j, b, jnp.where(ids == j + 1, -signed, F32(0.0)))
        full_ref[j] = out_ref_h
        hess_ref[j] = full_ref[j, local, :]
        refl_ref[j] = vec_ref[j, local, :]
        couple = [total(vec_ref[k] * u) for k in range(j)]
        for k in range(j):
            value = factor[k][k] * couple[k]
            for m in range(k + 1, j):
                value = value + factor[k][m] * couple[m]
            factor[k][j] = -value
        factor[j][j] = jnp.ones((1, 1), F32)
        if j + 1 < NB:
            edge = [vec_ref[k, 0:1, j + 1 : j + 2] for k in range(j + 1)]

        @pl.when(is_owner)
        def _():
            got_ref[j, pl.ds(col, 1)] = part_ref[
                j, pl.ds(pl.multiple_of(mine * SUB, SUB), SUB), :
            ][None]
            if j + 1 < NB:
                rest = mypan_ref[j + 1]
                for k in range(j):
                    rest = rest - ymine_ref[k] * edge[k]
            drop = jnp.zeros((SUB, LANES), F32)
            for k in range(j):
                drop = drop + ymine_ref[k] * couple[k]
            expect(got_ref.at[j, pl.ds(0, ncol - 1)], rs_sem.at[j])
            image = got_ref[j, 0]
            for i in range(1, ncol):
                image = image + got_ref[j, i]
            new_y = image - drop
            if j + 1 < NB:
                out_ref[j + 1] = rest - new_y * edge[j]
                gather(j + 1)
            ymine_ref[j] = new_y
            ydst = wy_ref.at[j, pl.ds(pl.multiple_of(mine * SUB, SUB), SUB)]
            peers_of_row(
                0,
                lambda to_row, to_col: send(
                    ymine_ref.at[j], ydst, y_send, y_sem, to_row, to_col
                ),
                True,
            )
            pltpu.make_async_copy(ymine_ref.at[j], ydst, y_sem).start()

    at_row = lax.broadcasted_iota(jnp.int32, (NB, NB), 0)
    at_col = lax.broadcasted_iota(jnp.int32, (NB, NB), 1)
    fac = jnp.zeros((NB, NB), F32)
    for k in range(NB):
        for m in range(k, NB):
            here = jnp.logical_and(at_row == k, at_col == m)
            fac = jnp.where(here, jnp.broadcast_to(factor[k][m], (NB, NB)), fac)
    fac_ref[...] = fac

    expect(wy_ref, y_sem)

    @pl.when(jnp.logical_not(is_owner))
    def _():
        expect(part_ref, rs_send)

    @pl.when(is_owner)
    def _():
        if owners > 1:
            expect(part_ref.at[:, pl.ds(0, (owners - 1) * SUB)], rs_send)
        for j in range(NB):
            expect(dummy_ref.at[pl.ds(0, (nrow * ncol - 1) * SUB)], ag_send.at[j])
        expect(dummy_ref.at[pl.ds(0, (ncol - 1) * SUB * NB)], y_send)

    if owners > 1:
        @pl.when(col == 0)
        def _():
            expect(pan_ref.at[:, pl.ds(0, (owners - 1) * SUB)], pan_send)


def shards(nrow, ncol, matrix):
    rows_local, cols_local = matrix.shape
    order = rows_local * nrow
    lines = rows_local // LANES
    tall = order // LANES
    blocks = rows_local // BLOCK
    panel = jax.ShapeDtypeStruct((NB, lines, LANES), F32)
    vmem = pl.BlockSpec(memory_space=pltpu.VMEM)
    dma = pltpu.SemaphoreType.DMA
    hess, refl, wy, fac = pl.pallas_call(
        functools.partial(kernel, nrow, ncol),
        out_shape=(panel, panel, panel, jax.ShapeDtypeStruct((NB, NB), F32)),
        in_specs=[pl.BlockSpec(memory_space=pl.ANY)],
        out_specs=(vmem, vmem, vmem, vmem),
        scratch_shapes=[
            pltpu.VMEM((rows_local, cols_local), F32),
            pltpu.VMEM((rows_local, LANES), F32),
            pltpu.VMEM((NB, lines, LANES), F32),
            pltpu.VMEM((NB, SUB, LANES), F32),
            pltpu.VMEM((NB, tall, LANES), F32),
            pltpu.VMEM((NB, tall, LANES), F32),
            pltpu.VMEM((NB, lines, LANES), F32),
            pltpu.VMEM((NB, ncol, SUB, LANES), F32),
            pltpu.VMEM((NB, SUB, LANES), F32),
            pltpu.VMEM((NB, SUB, LANES), F32),
            pltpu.VMEM((max(nrow * ncol - 1, (ncol - 1) * NB) * SUB, LANES), F32),
            dma((blocks,)),
            dma(()),
            dma(()),
            dma(()),
            dma(()),
            dma((NB,)),
            dma((NB,)),
            dma((NB,)),
            dma(()),
            dma(()),
        ],
        compiler_params=pltpu.CompilerParams(
            collective_id=0, has_side_effects=True, vmem_limit_bytes=56 * 2**20
        ),
    )(matrix)

    def lay(x):
        return x.reshape(NB, rows_local).T

    return lay(hess), lay(refl), lay(wy), fac


def solution(mesh):
    nrow, ncol = mesh.shape["row"], mesh.shape["col"]
    return jax.shard_map(
        functools.partial(shards, nrow, ncol),
        mesh=mesh,
        in_specs=(P("row", "col"),),
        out_specs=(P("row", None), P("row", None), P("row", None), P()),
        check_vma=False,
    )
```

time: 907 us -> 143 us (0.16); the launches traced: 898 us -> 143 us
  blocking collectives: 444 us -> 0 us
  matrix products: 265 us -> 0 us
  Pallas kernels: 0 us -> 138 us
  waiting for transfers between devices: 101 us -> 0 us
  between operations: 31.3 us -> 0.64 us
  other arithmetic: 27.4 us -> 0 us
  local copies, waits for them, and re-layouts: 28.4 us -> 4.73 us
    psum x31 -> x0, blocking collectives: 444 us -> none  [the longest x8 267 us: shards(): image = lax.psum(jnp.dot(matrix, piece, precision=exact), 'col')]
    dot_general x66 -> x0, matrix products: 265 us -> none  [the longest x8 246 us: shards(): image = lax.psum(jnp.dot(matrix, piece, precision=exact), 'col')]
    pallas_call x0 -> x1, Pallas kernels: none -> 138 us  [shards(): pl.pallas_call(functools.partial(kernel, nrow, ncol), out_shape=(panel, p...]
    psum x1 -> x0, waiting for transfers between devices: 101 us -> none  [spread(): return lax.psum(jnp.where(mine, value, jnp.zeros_like(value)), axis)]
    another operation x28 -> x0, other arithmetic: 18 us -> none
    slice x8 -> x0, local copies, waits for them, and re-layouts: 16.7 us -> none  [the longest x1 15.4 us: shards(): panel[:, column] - jnp.dot(wy_prod, refl_top[column], precision=exact)]
  transfers between devices with their start and end apart: 1 -> 0, of which waited for: 1 -> 0; matrix products, arithmetic and copies ran while one was open for 1% -> 0% of each run, Pallas kernels for 0% -> 0%
where the time goes in v1:
time: 143 us
  Pallas kernels  138 us (97%)
  local copies, waits for them, and re-layouts  4.73 us (3%)
    pallas_call x1, Pallas kernels, shards(): pl.pallas_call(functools.partial(kernel, nrow, ncol), out_shape=(panel, p...  138 us
    unnamed x2, local copies, waits for them, and re-layouts  2.91 us

profile of v1, /device:TPU:0, one launch (start us, length us, event | category | flops | bytes accessed | tf_op | source)
XLA Modules:
  0.0 143.0 jit_solution(11991027592468283937)
XLA Ops:
  0.6 137.7 %shard_map.46 = (f32[8,32,128]{2,1,0:T(8,128)}, f32[8,32,128]{2,1,0:T(8,128)}, f32[8,32,128]{2,1,0:T(8,128)}, f32[8,8]{1,0:T(8,128)}) custom-call(f32[4096,2048]{1,0:T(8,128)} %a_hbm.1), custom_call_target="tpu_custom_call" | custom-call | tf_op jit(solution)/shard_map/pallas_call | solution.py:280
  138.3 1.6 %copy.11 = f32[1,8,32,128]{3,1,2,0:T(8,128)} copy(f32[1,8,32,128]{3,2,1,0:T(8,128)} %bitcast.18) | data formatting | bytes 262144
  139.9 1.8 %bitcast_bitcast_fusion = (f32[4096,8]{0,1:T(8,128)}, f32[4096,8]{0,1:T(8,128)}) fusion(f32[1,8,32,128]{3,2,1,0:T(8,128)} %bitcast.20, f32[1,8,32,128]{3,2,1,0:T(8,128)} %bitcast.19), kind=kLoop, calls=%fused_computation | loop fusion | bytes 524288 | tf_op jit(solution)/shard_map/transpose | solution.py:314
  141.8 1.3 copy.13

commit v2 on v1

v2 whole, which is shorter than its diff:
```python
import functools

import jax
import jax.numpy as jnp
from jax import lax
from jax.experimental import pallas as pl
from jax.experimental.pallas import tpu as pltpu
from jax.sharding import PartitionSpec as P

NB = 8
LANES = 128
SUB = 8
STATS = 16
BLOCK = 256
F32 = jnp.float32
BF16 = jnp.bfloat16


def kernel(
    nrow, ncol, a_hbm, hess_ref, refl_ref, wy_ref, fac_ref,
    a_ref, first_ref, pan_ref, mypan_ref, part_ref, got_ref, stat_ref, stats_ref,
    vec_ref, yvec_ref,
    load_sem, first_sem, pan0_send, pan0_sem, pan_send, pan_sem, stat_send, stat_sem,
    part_send, part_sem, v_send, v_sem, y_send, y_sem,
):
    rows_local, cols_local = a_hbm.shape
    tiles = cols_local // LANES
    lines = rows_local // LANES
    split = rows_local // cols_local
    row, col = lax.axis_index("row"), lax.axis_index("col")
    blocks = rows_local // BLOCK

    def wrap(value, bound):
        return jnp.where(value >= bound, value - bound, value)

    def peers_of_row(dr, act, skip):
        to_row = wrap(row + dr, nrow)
        for dc in range(1 if skip else 0, ncol):
            act(to_row, wrap(col + dc, ncol))

    def block_load(i):
        span = pl.ds(i * BLOCK, BLOCK)
        return pltpu.make_async_copy(a_hbm.at[span], a_ref.at[span], load_sem.at[i])

    head = pltpu.make_async_copy(a_hbm.at[:, pl.ds(0, LANES)], first_ref, first_sem)

    @pl.when(col == 0)
    def _():
        head.start()

    for i in range(blocks):
        block_load(i).start()

    barrier = pltpu.get_barrier_semaphore()

    def greet(to_row, to_col):
        pl.semaphore_signal(
            barrier, inc=1, device_id=(to_row, to_col),
            device_id_type=pl.DeviceIdType.MESH,
        )

    def greet_row(dr, carry):
        peers_of_row(dr, greet, False)
        return carry

    lax.fori_loop(1, nrow, greet_row, 0)
    peers_of_row(0, greet, True)

    def send(src, dst, send_sem, recv_sem, to_row, to_col):
        pltpu.make_async_remote_copy(
            src_ref=src, dst_ref=dst, send_sem=send_sem, recv_sem=recv_sem,
            device_id=(to_row, to_col), device_id_type=pl.DeviceIdType.MESH,
        ).start()

    def place(src, dst, send_sem, recv_sem, to_row, to_col, here):
        @pl.when(here)
        def _():
            pltpu.make_async_copy(src, dst, recv_sem).start()

        @pl.when(jnp.logical_not(here))
        def _():
            send(src, dst, send_sem, recv_sem, to_row, to_col)

    def expect(ref, sem):
        pltpu.make_async_copy(ref, ref, sem).wait()

    def settle(ref, sem, here):
        count = ref.shape[1]

        @pl.when(jnp.logical_not(here))
        def _():
            expect(ref, sem)

        if count > 1:
            @pl.when(here)
            def _():
                expect(ref.at[:, pl.ds(0, count - 1)], sem)

    def spread(piece_of, dst, send_sem, recv_sem):
        for h in range(split):
            to_col = row * split + h
            for dr in range(nrow - 1, 0, -1):
                send(piece_of(h), dst, send_sem, recv_sem, wrap(row + dr, nrow), to_col)
            place(piece_of(h), dst, send_sem, recv_sem, row, to_col, to_col == col)

    @pl.when(col == 0)
    def _():
        head.wait()
        for h in range(split):
            def turn(t, carry):
                at = pl.multiple_of(h * cols_local + t * LANES, LANES)
                block = first_ref[pl.ds(at, LANES), :].T
                for k in range(NB + 1):
                    pan_ref[k, h, pl.ds(t, 1), :] = block[k : k + 1, :]
                return carry

            lax.fori_loop(0, tiles, turn, 0)

    pl.semaphore_wait(barrier, nrow * ncol - 1)

    @pl.when(col == 0)
    def _():
        spread(
            lambda h: pan_ref.at[pl.ds(0, 1), h], mypan_ref.at[pl.ds(0, 1)],
            pan0_send, pan0_sem,
        )
        spread(
            lambda h: pan_ref.at[pl.ds(1, NB), h], mypan_ref.at[pl.ds(1, NB)],
            pan_send, pan_sem,
        )

    ones = jnp.ones((SUB, 2 * LANES), BF16)

    def fold(acc, t, j):
        high = acc.astype(BF16)
        low = (acc - high.astype(F32)).astype(BF16)
        both = jnp.concatenate([high, low], axis=1)
        res = lax.dot_general(
            ones, both, (((1,), (1,)), ((), ())), preferred_element_type=F32
        )
        h = t // tiles
        part_ref[j, h, pl.ds(t - h * tiles, 1), :] = res[0:1, :]

    def matvec(j, vector):
        pieces = [
            jnp.broadcast_to(vector[t : t + 1, :], (SUB, LANES)) for t in range(tiles)
        ]

        def product(t):
            accs = []
            for s in range(LANES // SUB):
                at = pl.ds(pl.multiple_of(t * LANES + s * SUB, SUB), SUB)
                acc = a_ref[at, pl.ds(0, LANES)] * pieces[0]
                for p in range(1, tiles):
                    acc = acc + a_ref[at, pl.ds(p * LANES, LANES)] * pieces[p]
                accs.append(acc)
            return jnp.concatenate(accs, axis=0)

        per = BLOCK // LANES
        if j == 0:
            def loaded(i, carry):
                block_load(i).wait()
                for k in range(per):
                    fold(product(i * per + k), i * per + k, j)
                return carry

            lax.fori_loop(0, blocks, loaded, 0)
        else:
            def step(t, acc):
                fold(acc, t - 1, j)
                return product(t)

            fold(lax.fori_loop(1, lines, step, product(0)), lines - 1, j)

    owner = col // split
    slot = col - owner * split
    home = jnp.logical_and(owner == row, lax.rem(col, nrow) == row)

    def publish(src, ref, j, send_sem, recv_sem):
        for i in range(split):
            to_col = row + nrow * i
            here = jnp.logical_and(owner == row, to_col == col)
            place(src, ref.at[j, slot], send_sem, recv_sem, owner, to_col, here)

    lane = lax.broadcasted_iota(jnp.int32, (1, LANES), 1)
    line_ids = lax.broadcasted_iota(jnp.int32, (tiles, LANES), 0) * LANES
    ids = line_ids + lax.broadcasted_iota(jnp.int32, (tiles, LANES), 1)
    ids = ids + col * cols_local
    hess_ref[...] = jnp.zeros_like(hess_ref)

    factor = [[None] * NB for _ in range(NB)]
    gram = [[None] * NB for _ in range(NB)]
    tops = []
    images = []
    expect(mypan_ref.at[pl.ds(0, 1)], pan0_sem)
    b = mypan_ref[0]
    for j in range(NB):
        rows = [jnp.sum(vec_ref[k] * b, axis=0, keepdims=True) for k in range(j)]
        rows += [jnp.zeros((1, LANES), F32)] * (NB - j)
        rows.append(jnp.sum(b * b, axis=0, keepdims=True))
        rows.append(jnp.where(col == 0, b[0:1, :], F32(0.0)))
        rows += [jnp.zeros((1, LANES), F32)] * (STATS - NB - 2)
        stat = jnp.concatenate(rows, axis=0)
        stat_ref[j] = stat
        stats_ref[j, pl.ds(col, 1)] = stat[None]
        peers_of_row(
            0,
            lambda to_row, to_col: send(
                stat_ref.at[j], stats_ref.at[j, col], stat_send, stat_sem.at[j],
                to_row, to_col,
            ),
            True,
        )
        matvec(j, b)
        spread(lambda h: part_ref.at[j, h], got_ref.at[j, col], part_send, part_sem.at[j])

        expect(stats_ref.at[j, pl.ds(0, ncol - 1)], stat_sem.at[j])
        stat = stats_ref[j, 0]
        for i in range(1, ncol):
            stat = stat + stats_ref[j, i]
        sums = jnp.sum(stat, axis=1, keepdims=True)
        inner = [sums[k : k + 1, :] for k in range(j)]
        top = stat[NB + 1 : NB + 2, :]
        weight = []
        for m in range(j):
            value = factor[0][m] * inner[0]
            for k in range(1, m + 1):
                value = value + factor[k][m] * inner[k]
            weight.append(value)
        for m in range(j):
            top = top - tops[m] * weight[m]
        above = jnp.where(lane <= j, top, F32(0.0))
        square = sums[NB : NB + 1, :] - jnp.sum(above * above, axis=1, keepdims=True)
        norm = jnp.sqrt(square)
        alpha = top[:, j + 1 : j + 2]
        signed = jnp.where(alpha >= 0, norm, -norm)
        scale = 1.0 / jnp.sqrt(norm * (norm + jnp.abs(alpha)))
        u = b
        for m in range(j):
            u = u - vec_ref[m] * weight[m]
        u = jnp.where(ids > j, u, F32(0.0)) + jnp.where(ids == j + 1, signed, F32(0.0))
        u = u * scale
        vec_ref[j] = u
        publish(vec_ref.at[j], refl_ref, j, v_send, v_sem)
        vtop = jnp.where(lane > j, top, F32(0.0))
        vtop = (vtop + jnp.where(lane == j + 1, signed, F32(0.0))) * scale
        couple = []
        for k in range(j):
            value = inner[k]
            for m in range(j):
                value = value - gram[k][m] * weight[m]
            fix = jnp.where(lane == j + 1, signed, F32(0.0)) - above
            value = value + jnp.sum(tops[k] * fix, axis=1, keepdims=True)
            couple.append(value * scale)
        for k in range(j):
            value = factor[k][k] * couple[k]
            for m in range(k + 1, j):
                value = value + factor[k][m] * couple[m]
            factor[k][j] = -value
            gram[k][j] = couple[k]
            gram[j][k] = couple[k]
        factor[j][j] = jnp.ones((1, 1), F32)
        gram[j][j] = jnp.full((1, 1), 2.0, F32)
        tops.append(vtop)
        hrow = jnp.where(lane == j + 1, -signed, above)
        hess_ref[j, 0, 0:1, :] = jnp.where(row == 0, hrow, F32(0.0))
        if j == 0:
            expect(mypan_ref.at[pl.ds(1, NB)], pan_sem)
        drop = jnp.zeros((tiles, LANES), F32)
        for k in range(j):
            drop = drop + images[k] * weight[k]
        for i in range(j + 1):
            drop = drop + mypan_ref[i] * top[:, i : i + 1]
        drop = drop - mypan_ref[j + 1] * signed
        back = jnp.zeros((tiles, LANES), F32)
        for k in range(j):
            back = back + yvec_ref[k] * couple[k]
        if j + 1 < NB:
            rest = mypan_ref[j + 1]
            for k in range(j):
                rest = rest - yvec_ref[k] * tops[k][:, j + 1 : j + 2]

        expect(got_ref.at[j], part_sem.at[j])
        image = got_ref[j, 0]
        for i in range(1, ncol):
            image = image + got_ref[j, i]
        image = (image - drop) * scale
        images.append(image)
        new_y = image - back
        yvec_ref[j] = new_y
        if j + 1 < NB:
            b = rest - new_y * vtop[:, j + 1 : j + 2]
        publish(yvec_ref.at[j], wy_ref, j, y_send, y_sem)

    at_row = lax.broadcasted_iota(jnp.int32, (NB, NB), 0)
    at_col = lax.broadcasted_iota(jnp.int32, (NB, NB), 1)
    fac = jnp.zeros((NB, NB), F32)
    for k in range(NB):
        for m in range(k, NB):
            here = jnp.logical_and(at_row == k, at_col == m)
            fac = jnp.where(here, jnp.broadcast_to(factor[k][m], (NB, NB)), fac)
    fac_ref[...] = fac

    expect(refl_ref, v_sem)
    expect(wy_ref, y_sem)
    settle(got_ref, part_send, owner == row)
    settle(refl_ref, v_send, home)
    settle(wy_ref, y_send, home)
    expect(stats_ref.at[:, pl.ds(0, ncol - 1)], stat_send)

    @pl.when(col == 0)
    def _():
        settle(got_ref.at[pl.ds(0, 1)], pan0_send, row == 0)
        settle(got_ref, pan_send, row == 0)


def shards(nrow, ncol, matrix):
    rows_local, cols_local = matrix.shape
    tiles = cols_local // LANES
    split = rows_local // cols_local
    blocks = rows_local // BLOCK
    panel = jax.ShapeDtypeStruct((NB, split, tiles, LANES), F32)
    vmem = pl.BlockSpec(memory_space=pltpu.VMEM)
    dma = pltpu.SemaphoreType.DMA
    hess, refl, wy, fac = pl.pallas_call(
        functools.partial(kernel, nrow, ncol),
        out_shape=(panel, panel, panel, jax.ShapeDtypeStruct((NB, NB), F32)),
        in_specs=[pl.BlockSpec(memory_space=pl.ANY)],
        out_specs=(vmem, vmem, vmem, vmem),
        scratch_shapes=[
            pltpu.VMEM((rows_local, cols_local), F32),
            pltpu.VMEM((rows_local, LANES), F32),
            pltpu.VMEM((NB + 1, split, tiles, LANES), F32),
            pltpu.VMEM((NB + 1, tiles, LANES), F32),
            pltpu.VMEM((NB, split, tiles, LANES), F32),
            pltpu.VMEM((NB, ncol, tiles, LANES), F32),
            pltpu.VMEM((NB, STATS, LANES), F32),
            pltpu.VMEM((NB, ncol, STATS, LANES), F32),
            pltpu.VMEM((NB, tiles, LANES), F32),
            pltpu.VMEM((NB, tiles, LANES), F32),
            dma((blocks,)),
            dma(()),
            dma(()),
            dma(()),
            dma(()),
            dma(()),
            dma(()),
            dma((NB,)),
            dma(()),
            dma((NB,)),
            dma(()),
            dma(()),
            dma(()),
            dma(()),
        ],
        compiler_params=pltpu.CompilerParams(
            collective_id=0, has_side_effects=True, vmem_limit_bytes=56 * 2**20
        ),
    )(matrix)

    def lay(x):
        return x.reshape(NB, rows_local).T

    return lay(hess), lay(refl), lay(wy), fac


def solution(mesh):
    nrow, ncol = mesh.shape["row"], mesh.shape["col"]
    return jax.shard_map(
        functools.partial(shards, nrow, ncol),
        mesh=mesh,
        in_specs=(P("row", "col"),),
        out_specs=(P("row", None), P("row", None), P("row", None), P()),
        check_vma=False,
    )
```

time: 143 us -> 115 us (0.80)
  Pallas kernels: 138 us -> 110 us
    pallas_call x1, Pallas kernels: 138 us -> 110 us  [shards(): pl.pallas_call(functools.partial(kernel, nrow, ncol), out_shape=(panel, p...]
where the time goes in v2:
time: 115 us
  Pallas kernels  110 us (96%)
  local copies, waits for them, and re-layouts  4.73 us (4%)
    pallas_call x1, Pallas kernels, shards(): pl.pallas_call(functools.partial(kernel, nrow, ncol), out_shape=(panel, p...  110 us
    unnamed x2, local copies, waits for them, and re-layouts  2.91 us

profile of v2, /device:TPU:0, one launch (start us, length us, event | category | flops | bytes accessed | tf_op | source)
XLA Modules:
  0.0 115.2 jit_solution(1471476842203088142)
XLA Ops:
  0.6 109.8 %shard_map.46 = (f32[8,2,16,128]{3,2,1,0:T(8,128)}, f32[8,2,16,128]{3,2,1,0:T(8,128)}, f32[8,2,16,128]{3,2,1,0:T(8,128)}, f32[8,8]{1,0:T(8,128)}) custom-call(f32[4096,2048]{1,0:T(8,128)} %a_hbm.1), custom_call_target="tpu_custom_call" | custom-call | tf_op jit(solution)/shard_map/pallas_call | solution.py:325
  110.5 1.6 %copy.11 = f32[1,8,32,128]{3,1,2,0:T(8,128)} copy(f32[1,8,32,128]{3,2,1,0:T(8,128)} %bitcast.21) | data formatting | bytes 262144
  112.1 1.8 %bitcast_bitcast_fusion = (f32[4096,8]{0,1:T(8,128)}, f32[4096,8]{0,1:T(8,128)}) fusion(f32[1,8,32,128]{3,2,1,0:T(8,128)} %bitcast.23, f32[1,8,32,128]{3,2,1,0:T(8,128)} %bitcast.22), kind=kLoop, calls=%fused_computation | loop fusion | bytes 524288 | tf_op jit(solution)/shard_map/transpose | solution.py:362
  113.9 1.3 %copy.13 = f32[8,8]{1,0:T(8,128)} copy(f32[8,8]{1,0:T(8,128)} %get-tuple-element.21) | data formatting | bytes 512

commit v3 on v2

--- a/solution.py
+++ b/solution.py
@@ -49,7 +49,7 @@
         head.start()
 
     for i in range(blocks):
-        block_load(i).start()
+        block_load(i).start(priority=1)
 
     barrier = pltpu.get_barrier_semaphore()
 
@@ -211,6 +211,9 @@
             ),
             True,
         )
+        if j > 0:
+            publish(vec_ref.at[j - 1], refl_ref, j - 1, v_send, v_sem)
+            publish(yvec_ref.at[j - 1], wy_ref, j - 1, y_send, y_sem)
         matvec(j, b)
         spread(lambda h: part_ref.at[j, h], got_ref.at[j, col], part_send, part_sem.at[j])
 
@@ -241,7 +244,6 @@
         u = jnp.where(ids > j, u, F32(0.0)) + jnp.where(ids == j + 1, signed, F32(0.0))
         u = u * scale
         vec_ref[j] = u
-        publish(vec_ref.at[j], refl_ref, j, v_send, v_sem)
         vtop = jnp.where(lane > j, top, F32(0.0))
         vtop = (vtop + jnp.where(lane == j + 1, signed, F32(0.0))) * scale
         couple = []
@@ -286,12 +288,14 @@
             image = image + got_ref[j, i]
         image = (image - drop) * scale
         images.append(image)
+        if j + 1 == NB:
+            publish(vec_ref.at[j], refl_ref, j, v_send, v_sem)
         new_y = image - back
         yvec_ref[j] = new_y
         if j + 1 < NB:
             b = rest - new_y * vtop[:, j + 1 : j + 2]
-        publish(yvec_ref.at[j], wy_ref, j, y_send, y_sem)
-
+
+    publish(yvec_ref.at[NB - 1], wy_ref, NB - 1, y_send, y_sem)
     at_row = lax.broadcasted_iota(jnp.int32, (NB, NB), 0)
     at_col = lax.broadcasted_iota(jnp.int32, (NB, NB), 1)
     fac = jnp.zeros((NB, NB), F32)
@@ -312,6 +316,17 @@
     def _():
         settle(got_ref.at[pl.ds(0, 1)], pan0_send, row == 0)
         settle(got_ref, pan_send, row == 0)
+
+
+def finish(hess_in, refl_in, wy_in, fac_in, hess_out, refl_out, wy_out, fac_out):
+    split, tiles = hess_in.shape[1:3]
+    for src, dst in ((hess_in, hess_out), (refl_in, refl_out), (wy_in, wy_out)):
+        for h in range(split):
+            for t in range(tiles):
+                span = pl.ds((h * tiles + t) * LANES, LANES)
+                for k in range(NB):
+                    dst[k : k + 1, span] = src[k, h, t : t + 1, :]
+    fac_out[...] = fac_in[...]
 
 
 def shards(nrow, ncol, matrix):
@@ -358,10 +373,14 @@
         ),
     )(matrix)
 
-    def lay(x):
-        return x.reshape(NB, rows_local).T
-
-    return lay(hess), lay(refl), lay(wy), fac
+    flat = jax.ShapeDtypeStruct((NB, rows_local), F32)
+    hess, refl, wy, fac = pl.pallas_call(
+        finish,
+        out_shape=(flat, flat, flat, jax.ShapeDtypeStruct((NB, NB), F32)),
+        in_specs=[vmem] * 4,
+        out_specs=(vmem,) * 4,
+    )(hess, refl, wy, fac)
+    return hess.T, refl.T, wy.T, fac
 
 
 def solution(mesh):

time: 115 us -> 104 us (0.904)
  Pallas kernels: 110 us -> 103 us
  local copies, waits for them, and re-layouts: 4.73 us -> 0 us
    pallas_call x1, Pallas kernels: 110 us -> 101 us  [shards(): pl.pallas_call(functools.partial(kernel, nrow, ncol), out_shape=(panel, p...]
    unnamed x2 -> x0, local copies, waits for them, and re-layouts: 2.91 us -> none
    pallas_call x0 -> x1, Pallas kernels: none -> 2.05 us  [shards(): pl.pallas_call(finish, out_shape=(flat, flat, flat, jax.ShapeDtypeStruct(...]
    transpose x1 -> x0, local copies, waits for them, and re-layouts: 1.82 us -> none  [lay(): return x.reshape(NB, rows_local).T]
where the time goes in v3:
time: 104 us
  Pallas kernels  103 us (99%)
    pallas_call x1, Pallas kernels, shards(): pl.pallas_call(functools.partial(kernel, nrow, ncol), out_shape=(panel, p...  101 us

profile of v3, /device:TPU:0, one launch (start us, length us, event | category | flops | bytes accessed | tf_op | source)
XLA Modules:
  0.0 104.1 jit_solution(17913156637541041828)
XLA Ops:
  0.6 101.4 %shard_map.46 = (f32[8,2,16,128]{3,2,1,0:T(8,128)}, f32[8,2,16,128]{3,2,1,0:T(8,128)}, f32[8,2,16,128]{3,2,1,0:T(8,128)}, f32[8,8]{1,0:T(8,128)}) custom-call(f32[4096,2048]{1,0:T(8,128)} %a_hbm.1), custom_call_target="tpu_custom_call" | custom-call | tf_op jit(solution)/shard_map/pallas_call | solution.py:340
  102.0 2.0 %shard_map.47 = (f32[8,4096]{1,0:T(8,128)}, f32[8,4096]{1,0:T(8,128)}, f32[8,4096]{1,0:T(8,128)}, f32[8,8]{1,0:T(8,128)}) custom-call(f32[8,2,16,128]{3,2,1,0:T(8,128)} %get-tuple-element.12.hess_in, f32[8,2,16,128]{3,2,1,0:T(8,128)} %get-tuple-element.13.refl_in, f32[8,2,16,128]{3,2,1,0:T(8,128)} %get-tuple-element.14.wy_in, f32[8,8]{1,0:T(8,128)} %get-tuple-element.15.fac_in), custom_call_target="tpu_custom_call" | custom-call | tf_op jit(solution)/shard_map/pallas_call | solution.py:377
